TPU v7x, 32 devices: a whole 2x2x4 slice. The times are simulated.
32 devices in a mesh: gx: 4 (over z), gy: 8 (over y, x, core).
Axes of the slice: x: 2, y: 2, z: 4, core: 2. Of those that a mesh axis runs over, the one named last changes fastest.
Arguments:
- tables: float32 [2, 262144, 128], P(None, ('gx', 'gy')), may hold values from -0.9 to 0.9
- cold_rows: int32 [32, 2, 32, 16], P(('gx', 'gy')), may hold values from 0 to 8191, as said below
- cold_bags: int32 [32, 2, 32, 16], P(('gx', 'gy')), may hold values from -1 to 127, as said below
- hot_rows: int32 [2, 256], replicated, may hold values from 0 to 262143
- hot_ids: int32 [4096, 2, 8], P(('gx', 'gy')), may hold values from 0 to 255
Outputs:
- pooled: float32 [4096, 2, 128], P(('gx', 'gy'))
Inputs may be any that keep to these rules, and one draw needn't show every extreme that they name: `cold_rows`: every entry names one of the owner's 8192 rows. `cold_bags`: live slots of one sender, table and owner come first, the empty ones (-1) after them; in every draw each table has an owner whose 16 slots are all live from every sender.
All inputs are finite; a program needn't handle non-finite values.
Results may differ from a plain program's by a relative error of at most 0.0003.
Values sent between devices are 32-bit elements; how exact they have to be, the bound alone decides.
No kernel may reach another device: no remote copies, remote signals or barrier semaphores. Data moves between devices by JAX's collectives and lax.ppermute only.
A program may use at most 64 MiB of HBM per device.

v0:
```python
import math

import jax
import jax.numpy as jnp
from jax import lax
from jax.sharding import PartitionSpec as P


def pick_rows(table, indices):
    count = indices.shape[0]
    block = math.gcd(512, count)
    row_ids = jnp.arange(table.shape[0], dtype=jnp.int32)
    grouped = indices.reshape(count // block, block)

    def one_block(wanted):
        selector = (wanted[:, None] == row_ids[None, :]).astype(jnp.float32)
        return jnp.dot(
            selector, table, precision=lax.Precision.HIGHEST, preferred_element_type=jnp.float32
        )

    return lax.map(one_block, grouped).reshape(count, table.shape[1])


def body(tables, cold_rows, cold_bags, hot_rows, hot_ids):
    axis_x = lax.axis_size("gx")
    axis_y = lax.axis_size("gy")
    peer_count = axis_x * axis_y
    table_count, rows_dev, emb_width = tables.shape
    slot_cap = cold_rows.shape[3]
    batch_rows = hot_ids.shape[0]
    hot_count = hot_rows.shape[1]
    my_index = lax.axis_index(("gx", "gy"))
    hot_owner = hot_rows // rows_dev
    local_rows = jnp.where(hot_owner == my_index, hot_rows - my_index * rows_dev, -1)
    picked = jax.vmap(pick_rows)(tables, local_rows)
    hot_table = lax.psum(picked, ("gx", "gy"))
    matches = jnp.sum(
        (
            hot_ids[:, :, :, None] == jnp.arange(hot_count, dtype=jnp.int32)[None, None, None, :]
        ).astype(jnp.float32),
        axis=2,
    )
    hot_part = jnp.einsum("bth,thd->btd", matches, hot_table, precision=lax.Precision.HIGHEST)
    my_rows = cold_rows[0]
    my_bags = cold_bags[0]
    got_rows, got_bags = (
        lax.all_to_all(my_rows, ("gx", "gy"), split_axis=1, concat_axis=1, tiled=True),
        lax.all_to_all(my_bags, ("gx", "gy"), split_axis=1, concat_axis=1, tiled=True),
    )
    wanted_rows = jnp.where(got_bags >= 0, got_rows, -1)
    looked = jax.vmap(pick_rows)(tables, wanted_rows.reshape(table_count, -1))
    looked = looked.reshape(table_count, peer_count, slot_cap, emb_width)
    samples = jnp.arange(batch_rows, dtype=jnp.int32)
    returned = lax.all_to_all(looked, ("gx", "gy"), split_axis=1, concat_axis=1, tiled=True)
    onehot = (my_bags[:, None, :, :] == samples[None, :, None, None]).astype(jnp.float32)
    cold_part = jnp.einsum("tbpc,tpcd->btd", onehot, returned, precision=lax.Precision.HIGHEST)
    return cold_part + hot_part


def solution(mesh):
    return jax.shard_map(
        body,
        mesh=mesh,
        in_specs=(
            P(None, ("gx", "gy"), None),
            P(("gx", "gy"), None, None, None),
            P(("gx", "gy"), None, None, None),
            P(),
            P(("gx", "gy"), None, None),
        ),
        out_specs=P(("gx", "gy"), None, None),
        check_vma=False,
    )
```

profile of v0, /device:TPU:0, one launch (start us, length us, event | category | flops | bytes accessed | tf_op | source)
XLA Modules:
  0.0 203.2 jit_solution(9199264976657592994)
XLA Ops:
  6.5 1.4 copy.23
  7.9 7.3 %all-to-all-start.1 = ((s32[2,32,16]{2,0,1:T(2,128)}), s32[2,32,16]{2,0,1:T(2,128)S(1)}, u32[]{:S(2)}, u32[]{:S(2)}) async-start(s32[2,32,16]{2,0,1:T(2,128)} %bitcast.1), calls=%async_computation.1 | async-start | bytes 65536 | tf_op jit(solution)/shard_map/all_to_all | solution.py:47
  15.3 1.4 copy.22
  16.7 5.9 %all-to-all-done.1 = s32[2,32,16]{2,0,1:T(2,128)S(1)} async-done(((s32[2,32,16]{2,0,1:T(2,128)}), s32[2,32,16]{2,0,1:T(2,128)S(1)}, u32[]{:S(2)}, u32[]{:S(2)}) %all-to-all-start.1) | async-done | bytes 4128 | tf_op jit(solution)/shard_map/all_to_all | solution.py:47
  22.5 2.6 %all-to-all-start = ((s32[2,32,16]{2,0,1:T(2,128)}), s32[2,32,16]{2,0,1:T(2,128)S(1)}, u32[]{:S(2)}, u32[]{:S(2)}) async-start(s32[2,32,16]{2,0,1:T(2,128)} %bitcast), calls=%async_computation | async-start | bytes 65536 | tf_op jit(solution)/shard_map/all_to_all | solution.py:48
  25.1 7.2 %all-to-all-done = s32[2,32,16]{2,0,1:T(2,128)S(1)} async-done(((s32[2,32,16]{2,0,1:T(2,128)}), s32[2,32,16]{2,0,1:T(2,128)S(1)}, u32[]{:S(2)}, u32[]{:S(2)}) %all-to-all-start) | async-done | bytes 4128 | tf_op jit(solution)/shard_map/all_to_all | solution.py:48
  32.4 0.1 eq.74
  32.5 0.0 copy-start.1
  32.5 18.0 %fusion = f32[2,512,128]{2,1,0:T(8,128)S(1)} fusion(f32[2,8192,128]{2,1,0:T(8,128)} %param.5, s32[2,512]{1,0:T(2,128)S(1)} %eq.74), kind=kOutput, calls=%fused_computation.1 | convolution fusion | flops 12893290496 | bytes 8916992 | tf_op jit(solution)/shard_map/vmap()/while/body/eval_jaxpr/dot_general | solution.py:17
  50.5 0.0 copy-start
  50.5 0.9 copy.25
  51.4 2.6 %all-to-all-start.2 = ((f32[2,32,16,128]{3,2,0,1:T(8,128)}), f32[2,32,16,128]{3,2,0,1:T(8,128)S(1)}, u32[]{:S(2)}, u32[]{:S(2)}) async-start(f32[2,32,16,128]{3,2,0,1:T(8,128)} %copy.25), calls=%async_computation.2 | async-start | bytes 1048576 | tf_op jit(solution)/shard_map/all_to_all | solution.py:54
  54.0 0.2 all-reduce.2.cloned.1.call-start
  54.2 0.0 copy-done.1
  54.3 11.7 %fusion.2 = f32[2,256,128]{2,1,0:T(8,128)} fusion(f32[2,8192,128]{2,1,0:T(8,128)} %param.5, s32[2,256]{1,0:T(2,128)S(1)} %compare_select_fusion.1), kind=kOutput, calls=%fused_computation.4 | convolution fusion | flops 6446645248 | bytes 8652800 | tf_op jit(solution)/shard_map/vmap()/while/body/eval_jaxpr/dot_general | solution.py:17
  66.0 0.0 all-reduce.2.cloned.1.call-update
  66.0 0.0 copy-done
  66.0 0.1 copy.26
  66.2 0.8 convert_reduce_fusion
  67.0 2.6 %all-to-all-done.2 = f32[2,32,16,128]{3,2,0,1:T(8,128)S(1)} async-done(((f32[2,32,16,128]{3,2,0,1:T(8,128)}), f32[2,32,16,128]{3,2,0,1:T(8,128)S(1)}, u32[]{:S(2)}, u32[]{:S(2)}) %all-to-all-start.2) | async-done | bytes 524320 | tf_op jit(solution)/shard_map/all_to_all | solution.py:54
  69.6 1.5 convolution_bitcast_fusion
  71.1 122.8 %all-reduce.2.cloned.1.call-done = f32[2,256,128]{2,1,0:T(8,128)} async-done(((f32[2,256,128]{2,1,0:T(8,128)}), f32[2,256,128]{2,1,0:T(8,128)}) %all-reduce.2.cloned.1.call-update) | async-done | bytes 262160 | tf_op jit(solution)/shard_map/psum | solution.py:36
  194.0 1.6 fusion.4
  195.6 0.8 copy.29
  (3 shorter events, 0.0 us)
Async XLA Ops:
  7.9 14.6 %all-to-all-start.1 = ((s32[2,32,16]{2,0,1:T(2,128)}), s32[2,32,16]{2,0,1:T(2,128)S(1)}, u32[]{:S(2)}, u32[]{:S(2)}) async-start(s32[2,32,16]{2,0,1:T(2,128)} %bitcast.1), calls=%async_computation.1 | async-start | bytes 65536 | tf_op jit(solution)/shard_map/all_to_all | solution.py:47
  22.5 9.8 %all-to-all-start = ((s32[2,32,16]{2,0,1:T(2,128)}), s32[2,32,16]{2,0,1:T(2,128)S(1)}, u32[]{:S(2)}, u32[]{:S(2)}) async-start(s32[2,32,16]{2,0,1:T(2,128)} %bitcast), calls=%async_computation | async-start | bytes 65536 | tf_op jit(solution)/shard_map/all_to_all | solution.py:48
  32.5 21.8 %copy-start.1 = (s32[2,256]{1,0:T(2,128)S(1)}, s32[2,256]{1,0:T(2,128)}, u32[]{:S(2)}) copy-start(s32[2,256]{1,0:T(2,128)} %param.8) | copy-start | bytes 6148
  50.5 15.5 %copy-start = (s32[128,2,8]{0,2,1:T(8,128)S(1)}, s32[128,2,8]{0,2,1:T(8,128)}, u32[]{:S(2)}) copy-start(s32[128,2,8]{0,2,1:T(8,128)} %param.9) | copy-start | bytes 24580
  51.4 18.2 %all-to-all-start.2 = ((f32[2,32,16,128]{3,2,0,1:T(8,128)}), f32[2,32,16,128]{3,2,0,1:T(8,128)S(1)}, u32[]{:S(2)}, u32[]{:S(2)}) async-start(f32[2,32,16,128]{3,2,0,1:T(8,128)} %copy.25), calls=%async_computation.2 | async-start | bytes 1048576 | tf_op jit(solution)/shard_map/all_to_all | solution.py:54
  54.0 140.0 %all-reduce.2.cloned.1.call-start = ((), (), s32[]{:S(2)}) async-start(), calls=%async_computation.3 | async-start | bytes 524288 | tf_op jit(solution)/shard_map/psum | solution.py:36
Sparse Core Ops, SparseCore 0:
  66.1 127.7 all-reduce.1
where the time goes:
time: 204 us; the launch traced here: 203 us
  waiting for transfers between devices  139 us (68%)
  matrix products  32.8 us (16%)
  between operations  13.5 us (7%)
  starting transfers between devices  12.7 us (6%)
  local copies, waits for them, and re-layouts  4.66 us (2%)
    psum x1, waiting for transfers between devices, body(): hot_table = lax.psum(picked, ('gx', 'gy'))  123 us
    dot_general x2, matrix products, one_block(): jnp.dot(selector, table, precision=lax.Precision.HIGHEST, preferred_eleme...  29.7 us
    all_to_all x1, starting transfers between devices, body(): lax.all_to_all(my_rows, ('gx', 'gy'), split_axis=1, concat_axis=1, tiled=...  7.33 us
    all_to_all x1, waiting for transfers between devices, body(): lax.all_to_all(my_bags, ('gx', 'gy'), split_axis=1, concat_axis=1, tiled=...  7.25 us
    all_to_all x1, waiting for transfers between devices, body(): lax.all_to_all(my_rows, ('gx', 'gy'), split_axis=1, concat_axis=1, tiled=...  5.86 us
  transfers between devices with their start and end apart: 4, of which 4 were waited for; matrix products, arithmetic and copies ran while one was open for 8% of the time, Pallas kernels for 0%

commit v1 on v0

v1 whole, which is shorter than its diff:
```python
import jax
import jax.numpy as jnp
from jax import lax
from jax.experimental import pallas as pl
from jax.experimental.pallas import tpu as pltpu
from jax.sharding import PartitionSpec as P


AXES = ("gx", "gy")


def push_hot(peers, tables, hot_each, rows_dev, base_ref, hot_ref, index_ref, table_ref, out_ref, sem):
    chunk = tables * hot_each + 1
    out_ref[...] = jnp.zeros_like(out_ref)
    base = base_ref[0]

    def one_peer(peer, count):
        for t in range(tables):
            for s in range(hot_each):
                row = hot_ref[t, peer * hot_each + s] - base
                mine = jnp.logical_and(row >= 0, row < rows_dev)

                @pl.when(mine)
                def _():
                    pltpu.make_async_copy(
                        table_ref.at[t * rows_dev + row],
                        out_ref.at[peer * chunk + t * hot_each + s],
                        sem,
                    ).start()

                count = count + mine.astype(jnp.int32)
        out_ref[peer * chunk + chunk - 1] = index_ref[peer]
        return count

    count = lax.fori_loop(0, peers, one_peer, jnp.int32(0))

    @pl.when(count > 0)
    def _():
        pltpu.make_async_copy(
            table_ref.at[pl.ds(0, count)], out_ref.at[pl.ds(0, count)], sem
        ).wait()


def look_up(peers, tables, slots, hot_each, rows_dev, rows_ref, hot_ref, table_ref, out_ref, sem):
    cold = tables * slots
    hot = tables * hot_each
    chunk = cold + hot

    def one_peer(peer, carry):
        for t in range(tables):
            for c in range(slots):
                row = rows_ref[peer, t * slots + c]
                pltpu.make_async_copy(
                    table_ref.at[t * rows_dev + row],
                    out_ref.at[peer * chunk + t * slots + c],
                    sem,
                ).start()
        return carry

    lax.fori_loop(0, peers, one_peer, 0)
    total = hot_ref[0, pl.ds(0, hot)]
    for peer in range(1, peers):
        total = total + hot_ref[peer, pl.ds(0, hot)]
    for peer in range(peers):
        out_ref[pl.ds(peer * chunk + cold, hot)] = total
    pltpu.make_async_copy(
        table_ref.at[pl.ds(0, peers * cold)], out_ref.at[pl.ds(0, peers * cold)], sem
    ).wait()


def pool(tables, bags_ref, names_ref, ids_ref, rows_ref, out_ref):
    batch = out_ref.shape[0]
    count = rows_ref.shape[0]
    sample = lax.broadcasted_iota(jnp.int32, (batch, count), 0)
    picks = []
    for t in range(tables):
        hits = (bags_ref[pl.ds(t, 1), :] == sample).astype(jnp.float32)
        names = names_ref[pl.ds(t, 1), :]
        for k in range(ids_ref.shape[2]):
            hits = hits + (ids_ref[t, :, k : k + 1] == names).astype(jnp.float32)
        picks.append(hits.astype(jnp.bfloat16))
    rows = rows_ref[...]
    high = rows.astype(jnp.bfloat16)
    rest = rows - high.astype(jnp.float32)
    mid = rest.astype(jnp.bfloat16)
    low = (rest - mid.astype(jnp.float32)).astype(jnp.bfloat16)
    for t in range(tables):
        part = jnp.dot(picks[t], low, preferred_element_type=jnp.float32)
        part = part + jnp.dot(picks[t], mid, preferred_element_type=jnp.float32)
        part = part + jnp.dot(picks[t], high, preferred_element_type=jnp.float32)
        out_ref[:, t, :] = part


def body(tables, cold_rows, cold_bags, hot_rows, hot_ids):
    peers = lax.axis_size("gx") * lax.axis_size("gy")
    table_count, rows_dev, width = tables.shape
    slots = cold_rows.shape[3]
    batch = hot_ids.shape[0]
    hot_count = hot_rows.shape[1]
    hot_each = -(-hot_count // peers)
    cold = table_count * slots
    hot = table_count * hot_each
    base = (lax.axis_index(AXES) * rows_dev).astype(jnp.int32).reshape(1)
    hot_rows = jnp.pad(hot_rows, ((0, 0), (0, hot_each * peers - hot_count)), constant_values=-1)
    flat = tables.reshape(table_count * rows_dev, 1, width)
    lanes = -(-cold // width)
    assert lanes == 1
    wanted = jnp.transpose(cold_rows[0], (1, 0, 2)).reshape(peers, 1, cold).astype(jnp.float32)
    wanted = jnp.pad(wanted, ((0, 0), (0, 0), (0, width - cold)))

    smem = pl.BlockSpec(memory_space=pltpu.SMEM)
    vmem = pl.BlockSpec(memory_space=pltpu.VMEM)
    anywhere = pl.BlockSpec(memory_space=pl.ANY)

    first = pl.pallas_call(
        lambda *refs: push_hot(peers, table_count, hot_each, rows_dev, *refs),
        out_shape=jax.ShapeDtypeStruct((peers * (hot + 1), 1, width), jnp.float32),
        in_specs=[smem, smem, vmem, anywhere],
        out_specs=vmem,
        scratch_shapes=[pltpu.SemaphoreType.DMA],
        name="push_hot",
    )(base, hot_rows, wanted, flat)
    first = first.reshape(peers, hot + 1, 1, width)
    first = lax.all_to_all(first, AXES, split_axis=0, concat_axis=0, tiled=True)
    asked = first[:, hot, 0, :cold].astype(jnp.int32)

    second = pl.pallas_call(
        lambda *refs: look_up(peers, table_count, slots, hot_each, rows_dev, *refs),
        out_shape=jax.ShapeDtypeStruct((peers * (cold + hot), 1, width), jnp.float32),
        in_specs=[smem, vmem, anywhere],
        out_specs=vmem,
        scratch_shapes=[pltpu.SemaphoreType.DMA],
        name="look_up",
    )(asked, first, flat)
    second = second.reshape(peers, cold + hot, 1, width)
    second = lax.all_to_all(second, AXES, split_axis=0, concat_axis=0, tiled=True)
    second = second.reshape(peers * (cold + hot), width)

    slot_table = jnp.arange(cold + hot, dtype=jnp.int32)
    bags = []
    names = []
    for t in range(table_count):
        bags.append(jnp.pad(cold_bags[0, t], ((0, 0), (t * slots, cold + hot - (t + 1) * slots)), constant_values=-1).reshape(-1))
        place = slot_table - cold - t * hot_each
        inside = jnp.logical_and(place >= 0, place < hot_each)
        peer = jnp.arange(peers, dtype=jnp.int32)[:, None]
        names.append(jnp.where(inside[None, :], peer * hot_each + place[None, :], -1).reshape(-1))
    return pl.pallas_call(
        lambda *refs: pool(table_count, *refs),
        out_shape=jax.ShapeDtypeStruct((batch, table_count, width), jnp.float32),
        in_specs=[vmem] * 4,
        out_specs=vmem,
        name="pool",
    )(jnp.stack(bags), jnp.stack(names), jnp.transpose(hot_ids, (1, 0, 2)), second)


def solution(mesh):
    return jax.shard_map(
        body,
        mesh=mesh,
        in_specs=(
            P(None, AXES, None),
            P(AXES, None, None, None),
            P(AXES, None, None, None),
            P(),
            P(AXES, None, None),
        ),
        out_specs=P(AXES, None, None),
        check_vma=False,
    )
```

time: 204 us -> 60.9 us (0.30)
  waiting for transfers between devices: 139 us -> 17.8 us
  matrix products: 32.8 us -> 0 us
  blocking collectives: 0 us -> 18.8 us
  Pallas kernels: 0 us -> 15.5 us
  between operations: 13.5 us -> 0.1 us
  starting transfers between devices: 12.7 us -> 2.64 us
    psum x1 -> x0, waiting for transfers between devices: 123 us -> none  [body(): hot_table = lax.psum(picked, ('gx', 'gy'))]
    dot_general x4 -> x0, matrix products: 32.8 us -> none  [the longest x2 29.7 us: one_block(): jnp.dot(selector, table, precision=lax.Precision.HIGHEST, preferred_eleme...]
    all_to_all x0 -> x1, blocking collectives: none -> 18.8 us  [body(): first = lax.all_to_all(first, AXES, split_axis=0, concat_axis=0, tiled=True)]
    pallas_call x0 -> x3, Pallas kernels: none -> 15.5 us  [the longest x1 6.66 us: body(): pl.pallas_call(lambda *refs: look_up(peers, table_count, slots, hot_each,...]
    all_to_all x3 -> x1, starting transfers between devices: 12.5 us -> 2.64 us  [body(): lax.all_to_all(second, AXES, split_axis=0, concat_axis=0, tiled=True)]
    all_to_all x3 -> x1, waiting for transfers between devices: 15.7 us -> 17.8 us  [body(): lax.all_to_all(second, AXES, split_axis=0, concat_axis=0, tiled=True)]
  transfers between devices with their start and end apart: 4 -> 1, of which waited for: 4 -> 1; matrix products, arithmetic and copies ran while one was open for 8% -> 4% of each run, Pallas kernels for 0% -> 0%
where the time goes in v1:
time: 60.9 us; the launch traced here: 60.5 us
  blocking collectives  18.8 us (31%)
  waiting for transfers between devices  17.8 us (29%)
  Pallas kernels  15.5 us (25%)
  local copies, waits for them, and re-layouts  2.98 us (5%)
  other arithmetic  2.69 us (4%)
  starting transfers between devices  2.64 us (4%)
    all_to_all x1, blocking collectives, body(): first = lax.all_to_all(first, AXES, split_axis=0, concat_axis=0, tiled=True)  18.8 us
    all_to_all x1, waiting for transfers between devices, body(): lax.all_to_all(second, AXES, split_axis=0, concat_axis=0, tiled=True)  17.8 us
    pallas_call x1, Pallas kernels, body(): pl.pallas_call(lambda *refs: look_up(peers, table_count, slots, hot_each,...  6.66 us
    pallas_call x1, Pallas kernels, body(): pl.pallas_call(lambda *refs: push_hot(peers, table_count, hot_each, rows_...  4.87 us
    pallas_call x1, Pallas kernels, body(): pl.pallas_call(lambda *refs: pool(table_count, *refs), out_shape=jax.Shap...  3.98 us
    all_to_all x1, starting transfers between devices, body(): lax.all_to_all(second, AXES, split_axis=0, concat_axis=0, tiled=True)  2.64 us
    unnamed x11, local copies, waits for them, and re-layouts  1.86 us
  transfers between devices with their start and end apart: 1, of which 1 were waited for; matrix products, arithmetic and copies ran while one was open for 4% of the time, Pallas kernels for 0%

profile of v1, /device:TPU:0, one launch (start us, length us, event | category | flops | bytes accessed | tf_op | source)
XLA Modules:
  0.0 60.5 jit_solution(11753050038571324072)
XLA Ops:
  0.0 0.7 %convert_element_type.27 = f32[1,2,32,16]{2,3,1,0:T(8,128)S(1)} convert(s32[1,2,32,16]{2,3,1,0:T(8,128)} %param.6) | non-fusion elementwise | flops 1024 | bytes 8192 | tf_op jit(solution)/shard_map/convert_element_type | solution.py:108
  0.7 0.1 copy.17
  0.8 0.6 %pad.14.refs_2_ = f32[32,1,128]{2,1,0:T(1,128)} pad(f32[32,1,32]{2,1,0:T(1,128)S(1)} %copy.17, f32[]{:T(128)} %constant.26.clone.1), padding=0_0x0_0x0_96 | pad | bytes 20484 | tf_op jit(solution)/shard_map/jit(_pad)/pad | solution.py:109
  1.4 0.0 copy-start.2
  1.4 0.0 copy-start.3
  1.4 4.9 %push_hot.1 = f32[544,1,128]{2,1,0:T(1,128)} custom-call(s32[1]{0:T(128)} %bitcast.3.refs_0_, s32[2,256]{1,0:T(2,128)} %refs_1_.1, f32[32,1,128]{2,1,0:T(1,128)} %pad.14.refs_2_, f32[16384,1,128]{2,1,0:T(1,128)} %bitcast.18), custom_call_target="tpu_custom_call" | custom-call | tf_op jit(solution)/shard_map/push_hot/pallas_call | solution.py:115
  6.3 18.8 %all_to_all.10.refs_1_ = f32[32,17,1,128]{3,2,1,0:T(1,128)S(1)} all-to-all(f32[32,17,1,128]{3,2,1,0:T(1,128)} %bitcast.22), channel_id=1, replica_groups=mesh['gx'=4,'gy'=8] {'gx','gy'}, dimensions={0} | all-to-all | bytes 557056 | tf_op jit(solution)/shard_map/all_to_all | solution.py:124
  25.1 0.0 copy-start.1
  25.1 0.7 %slice_convert_fusion = s32[32,1,1,32]{3,2,1,0:T(1,128)} fusion(f32[32,17,1,128]{3,2,1,0:T(1,128)S(1)} %all_to_all.10.refs_1_), kind=kLoop, calls=%fused_computation | loop fusion | flops 1024 | bytes 8192 | tf_op jit(solution)/shard_map/convert_element_type | solution.py:125
  25.7 0.0 copy-done.1
  25.8 6.7 %look_up.1 = f32[1536,1,128]{2,1,0:T(1,128)} custom-call(s32[32,32]{1,0:T(8,128)} %bitcast.24, f32[32,17,1,128]{3,2,1,0:T(1,128)} %copy-done.1, f32[16384,1,128]{2,1,0:T(1,128)} %bitcast.19), custom_call_target="tpu_custom_call" | custom-call | tf_op jit(solution)/shard_map/look_up/pallas_call | solution.py:127
  32.4 2.6 %all-to-all-start.1 = ((f32[32,48,1,128]{3,1,2,0:T(8,128)}), f32[32,48,1,128]{3,1,2,0:T(8,128)S(1)}, u32[]{:S(2)}, u32[]{:S(2)}) async-start(f32[32,48,1,128]{3,1,2,0:T(8,128)} %bitcast.20), calls=%async_computation.1 | async-start | bytes 1572864 | tf_op jit(solution)/shard_map/all_to_all | solution.py:136
  35.1 0.1 add_select_fusion.1
  35.2 0.1 select_n.28
  35.3 0.1 select_n.30
  35.4 0.0 copy-done.2
  35.4 0.1 copy.19
  35.5 0.1 stack_reshape.8
  35.6 0.1 copy.20
  35.6 0.1 pad.13.clone
  35.7 0.1 stack_reshape.9
  35.8 0.0 copy-done.3
  35.8 0.8 %copy.16 = s32[128,2,8]{2,0,1:T(8,128)} copy(s32[128,2,8]{0,2,1:T(8,128)S(1)} %copy-done.3) | data formatting | bytes 16384 | tf_op args[4]
  36.6 0.6 %pad_add_fusion.1.refs_1_ = s32[2,1536]{1,0:T(2,128)} fusion(s32[1,1536]{1,0:T(1,128)S(1)} %select_n.30, s32[1,1536]{1,0:T(1,128)S(1)} %select_n.28), kind=kLoop, calls=%fused_computation.4 | loop fusion | flops 3072 | bytes 24576 | tf_op jit(solution)/shard_map/stack | solution.py:154
  37.2 0.6 %pad_add_fusion.refs_0_ = s32[2,1536]{1,0:T(2,128)} fusion(s32[1,1536]{1,0:T(1,128)S(1)} %stack_reshape.9, s32[1,1536]{1,0:T(1,128)S(1)} %stack_reshape.8), kind=kLoop, calls=%fused_computation.3 | loop fusion | flops 3072 | bytes 24576 | tf_op jit(solution)/shard_map/stack | solution.py:154
  37.8 17.8 %all-to-all-done.1 = f32[32,48,1,128]{3,1,2,0:T(8,128)S(1)} async-done(((f32[32,48,1,128]{3,1,2,0:T(8,128)}), f32[32,48,1,128]{3,1,2,0:T(8,128)S(1)}, u32[]{:S(2)}, u32[]{:S(2)}) %all-to-all-start.1) | async-done | bytes 786464 | tf_op jit(solution)/shard_map/all_to_all | solution.py:136
  55.7 0.0 copy-start
  55.7 0.9 %copy-done = f32[32,48,1,128]{3,1,2,0:T(8,128)} copy-done((f32[32,48,1,128]{3,1,2,0:T(8,128)}, f32[32,48,1,128]{3,1,2,0:T(8,128)S(1)}, u32[]{:S(2)}) %copy-start) | copy-done | bytes 786456
  56.5 4.0 %pool.1 = f32[128,2,128]{2,1,0:T(2,128)} custom-call(s32[2,1536]{1,0:T(2,128)} %pad_add_fusion.refs_0_, s32[2,1536]{1,0:T(2,128)} %pad_add_fusion.1.refs_1_, s32[2,128,8]{2,1,0:T(8,128)} %bitcast.23, f32[1536,128]{1,0:T(8,128)} %bitcast.21), custom_call_target="tpu_custom_call" | custom-call | tf_op jit(solution)/shard_map/pool/pallas_call | solution.py:148
  (5 shorter events, 0.0 us)
Async XLA Ops:
  1.4 33.9 %copy-start.2 = (s32[1,2,32,16]{2,3,1,0:T(8,128)S(1)}, s32[1,2,32,16]{2,3,1,0:T(8,128)}, u32[]{:S(2)}) copy-start(s32[1,2,32,16]{2,3,1,0:T(8,128)} %param.7) | copy-start | bytes 12292
  1.4 34.4 %copy-start.3 = (s32[128,2,8]{0,2,1:T(8,128)S(1)}, s32[128,2,8]{0,2,1:T(8,128)}, u32[]{:S(2)}) copy-start(s32[128,2,8]{0,2,1:T(8,128)} %param.9) | copy-start | bytes 24580
  25.1 0.7 %copy-start.1 = (f32[32,17,1,128]{3,2,1,0:T(1,128)}, f32[32,17,1,128]{3,2,1,0:T(1,128)S(1)}, u32[]{:S(2)}) copy-start(f32[32,17,1,128]{3,2,1,0:T(1,128)S(1)} %all_to_all.10.refs_1_) | copy-start | bytes 835588
  32.4 23.2 %all-to-all-start.1 = ((f32[32,48,1,128]{3,1,2,0:T(8,128)}), f32[32,48,1,128]{3,1,2,0:T(8,128)S(1)}, u32[]{:S(2)}, u32[]{:S(2)}) async-start(f32[32,48,1,128]{3,1,2,0:T(8,128)} %bitcast.20), calls=%async_computation.1 | async-start | bytes 1572864 | tf_op jit(solution)/shard_map/all_to_all | solution.py:136
  55.7 0.9 %copy-start = (f32[32,48,1,128]{3,1,2,0:T(8,128)}, f32[32,48,1,128]{3,1,2,0:T(8,128)S(1)}, u32[]{:S(2)}) copy-start(f32[32,48,1,128]{3,1,2,0:T(8,128)S(1)} %all-to-all-done.1) | copy-start | bytes 2359300

commit v2 on v1

--- a/solution.py
+++ b/solution.py
@@ -68,26 +68,28 @@
     ).wait()
 
 
-def pool(tables, bags_ref, names_ref, ids_ref, rows_ref, out_ref):
-    batch = out_ref.shape[0]
-    count = rows_ref.shape[0]
+def select(tables, bags_ref, names_ref, ids_ref, pick_ref):
+    batch, count = pick_ref.shape[1:]
     sample = lax.broadcasted_iota(jnp.int32, (batch, count), 0)
-    picks = []
     for t in range(tables):
         hits = (bags_ref[pl.ds(t, 1), :] == sample).astype(jnp.float32)
         names = names_ref[pl.ds(t, 1), :]
         for k in range(ids_ref.shape[2]):
             hits = hits + (ids_ref[t, :, k : k + 1] == names).astype(jnp.float32)
-        picks.append(hits.astype(jnp.bfloat16))
+        pick_ref[t] = hits.astype(jnp.bfloat16)
+
+
+def pool(tables, pick_ref, rows_ref, out_ref):
     rows = rows_ref[...]
     high = rows.astype(jnp.bfloat16)
     rest = rows - high.astype(jnp.float32)
     mid = rest.astype(jnp.bfloat16)
     low = (rest - mid.astype(jnp.float32)).astype(jnp.bfloat16)
     for t in range(tables):
-        part = jnp.dot(picks[t], low, preferred_element_type=jnp.float32)
-        part = part + jnp.dot(picks[t], mid, preferred_element_type=jnp.float32)
-        part = part + jnp.dot(picks[t], high, preferred_element_type=jnp.float32)
+        pick = pick_ref[t]
+        part = jnp.dot(pick, low, preferred_element_type=jnp.float32)
+        part = part + jnp.dot(pick, mid, preferred_element_type=jnp.float32)
+        part = part + jnp.dot(pick, high, preferred_element_type=jnp.float32)
         out_ref[:, t, :] = part
 
 
@@ -111,6 +113,7 @@
     smem = pl.BlockSpec(memory_space=pltpu.SMEM)
     vmem = pl.BlockSpec(memory_space=pltpu.VMEM)
     anywhere = pl.BlockSpec(memory_space=pl.ANY)
+    small = pltpu.CompilerParams(vmem_limit_bytes=24 * 1024 * 1024)
 
     first = pl.pallas_call(
         lambda *refs: push_hot(peers, table_count, hot_each, rows_dev, *refs),
@@ -145,13 +148,24 @@
         inside = jnp.logical_and(place >= 0, place < hot_each)
         peer = jnp.arange(peers, dtype=jnp.int32)[:, None]
         names.append(jnp.where(inside[None, :], peer * hot_each + place[None, :], -1).reshape(-1))
+    count = peers * (cold + hot)
+    picks = pl.pallas_call(
+        lambda *refs: select(table_count, *refs),
+        out_shape=jax.ShapeDtypeStruct((table_count, batch, count), jnp.bfloat16),
+        in_specs=[vmem] * 3,
+        out_specs=vmem,
+        compiler_params=small,
+        cost_estimate=pl.CostEstimate(flops=40 * batch * count * table_count, bytes_accessed=4 * batch * count, transcendentals=0),
+        name="select",
+    )(jnp.stack(bags), jnp.stack(names), jnp.transpose(hot_ids, (1, 0, 2)))
     return pl.pallas_call(
         lambda *refs: pool(table_count, *refs),
         out_shape=jax.ShapeDtypeStruct((batch, table_count, width), jnp.float32),
-        in_specs=[vmem] * 4,
+        in_specs=[vmem] * 2,
         out_specs=vmem,
+        compiler_params=small,
         name="pool",
-    )(jnp.stack(bags), jnp.stack(names), jnp.transpose(hot_ids, (1, 0, 2)), second)
+    )(picks, second)
 
 
 def solution(mesh):

time: 60.9 us -> 57.5 us (0.944)
  local copies, waits for them, and re-layouts: 2.98 us -> 1.45 us
  other arithmetic: 2.69 us -> 1.5 us
    pallas_call x1, Pallas kernels: 3.98 us -> 1.48 us  [body(): pl.pallas_call(lambda *refs: pool(table_count, *refs), out_shape=jax.Shap...]
    pallas_call x0 -> x1, Pallas kernels: none -> 1.54 us  [body(): pl.pallas_call(lambda *refs: select(table_count, *refs), out_shape=jax.Sh...]
    unnamed x11 -> x9, local copies, waits for them, and re-layouts: 1.86 us -> 0.33 us
  transfers between devices with their start and end apart: 1 -> 1, of which waited for: 1 -> 1; matrix products, arithmetic and copies ran while one was open for 4% -> 1% of each run, Pallas kernels for 0% -> 3%
where the time goes in v2:
time: 57.5 us; the launch traced here: 57.2 us
  blocking collectives  18.4 us (32%)
  waiting for transfers between devices  18.1 us (31%)
  Pallas kernels  14.9 us (26%)
  starting transfers between devices  2.64 us (5%)
  other arithmetic  1.5 us (3%)
  local copies, waits for them, and re-layouts  1.45 us (3%)
    all_to_all x1, blocking collectives, body(): first = lax.all_to_all(first, AXES, split_axis=0, concat_axis=0, tiled=True)  18.4 us
    all_to_all x1, waiting for transfers between devices, body(): lax.all_to_all(second, AXES, split_axis=0, concat_axis=0, tiled=True)  18.1 us
    pallas_call x1, Pallas kernels, body(): pl.pallas_call(lambda *refs: look_up(peers, table_count, slots, hot_each,...  6.66 us
    pallas_call x1, Pallas kernels, body(): pl.pallas_call(lambda *refs: push_hot(peers, table_count, hot_each, rows_...  5.23 us
    all_to_all x1, starting transfers between devices, body(): lax.all_to_all(second, AXES, split_axis=0, concat_axis=0, tiled=True)  2.64 us
    pallas_call x1, Pallas kernels, body(): pl.pallas_call(lambda *refs: select(table_count, *refs), out_shape=jax.Sh...  1.54 us
    pallas_call x1, Pallas kernels, body(): pl.pallas_call(lambda *refs: pool(table_count, *refs), out_shape=jax.Shap...  1.48 us
  transfers between devices with their start and end apart: 1, of which 1 were waited for; matrix products, arithmetic and copies ran while one was open for 1% of the time, Pallas kernels for 3%

profile of v2, /device:TPU:0, one launch (start us, length us, event | category | flops | bytes accessed | tf_op | source)
XLA Modules:
  0.0 57.2 jit_solution(5726689583441479264)
XLA Ops:
  0.0 0.7 %convert_element_type.27 = f32[1,2,32,16]{2,3,1,0:T(8,128)S(1)} convert(s32[1,2,32,16]{2,3,1,0:T(8,128)} %param.6) | non-fusion elementwise | flops 1024 | bytes 8192 | tf_op jit(solution)/shard_map/convert_element_type | solution.py:110
  0.7 0.1 copy.17
  0.8 0.6 %pad.14.refs_2_ = f32[32,1,128]{2,1,0:T(1,128)} pad(f32[32,1,32]{2,1,0:T(1,128)S(1)} %copy.17, f32[]{:T(128)} %constant.26.clone.1), padding=0_0x0_0x0_96 | pad | bytes 20484 | tf_op jit(solution)/shard_map/jit(_pad)/pad | solution.py:111
  1.4 0.0 copy-start.1
  1.4 0.0 copy-start.2
  1.4 5.2 %push_hot.1 = f32[544,1,128]{2,1,0:T(1,128)} custom-call(s32[1]{0:T(128)} %bitcast.3.refs_0_, s32[2,256]{1,0:T(2,128)} %refs_1_.1, f32[32,1,128]{2,1,0:T(1,128)} %pad.14.refs_2_, f32[16384,1,128]{2,1,0:T(1,128)} %bitcast.20), custom_call_target="tpu_custom_call" | custom-call | tf_op jit(solution)/shard_map/push_hot/pallas_call | solution.py:118
  6.7 18.4 %all_to_all.10.refs_1_ = f32[32,17,1,128]{3,2,1,0:T(1,128)S(1)} all-to-all(f32[32,17,1,128]{3,2,1,0:T(1,128)} %bitcast.23), channel_id=1, replica_groups=mesh['gx'=4,'gy'=8] {'gx','gy'}, dimensions={0} | all-to-all | bytes 557056 | tf_op jit(solution)/shard_map/all_to_all | solution.py:127
  25.1 0.0 copy-start
  25.1 0.7 %slice_convert_fusion = s32[32,1,1,32]{3,2,1,0:T(1,128)} fusion(f32[32,17,1,128]{3,2,1,0:T(1,128)S(1)} %all_to_all.10.refs_1_), kind=kLoop, calls=%fused_computation | loop fusion | flops 1024 | bytes 8192 | tf_op jit(solution)/shard_map/convert_element_type | solution.py:128
  25.8 0.0 copy-done
  25.8 6.7 %look_up.1 = f32[1536,1,128]{2,1,0:T(1,128)} custom-call(s32[32,32]{1,0:T(8,128)} %bitcast.24, f32[32,17,1,128]{3,2,1,0:T(1,128)} %copy-done, f32[16384,1,128]{2,1,0:T(1,128)} %bitcast.21), custom_call_target="tpu_custom_call" | custom-call | tf_op jit(solution)/shard_map/look_up/pallas_call | solution.py:130
  32.5 2.6 %all-to-all-start.1 = ((f32[32,48,1,128]{3,1,2,0:T(8,128)}), f32[32,48,1,128]{3,1,2,0:T(8,128)S(1)}, u32[]{:S(2)}, u32[]{:S(2)}) async-start(f32[32,48,1,128]{3,1,2,0:T(8,128)} %bitcast.22), calls=%async_computation.1 | async-start | bytes 1572864 | tf_op jit(solution)/shard_map/all_to_all | solution.py:139
  35.1 0.0 copy-done.1
  35.1 0.1 copy.19
  35.2 0.1 stack_reshape.8
  35.3 0.1 copy.20
  35.4 0.1 pad.13.clone
  35.5 0.1 stack_reshape.9
  35.6 0.1 add_select_fusion.1
  35.7 0.1 select_n.28
  35.8 0.1 select_n.30
  35.8 0.0 copy-done.2
  35.9 0.1 copy.16
  36.0 1.5 %select.4.refs_0_ = bf16[2,128,1536]{2,1,0:T(8,128)(2,1)S(1)} custom-call(s32[2,1536]{1,0:T(2,128)S(1)} %pad_add_fusion.refs_0_, s32[2,1536]{1,0:T(2,128)S(1)} %pad_add_fusion.1.refs_1_, s32[2,128,8]{2,1,0:T(8,128)S(1)} %bitcast.19), custom_call_target="tpu_custom_call" | custom-call | flops 15728640 | bytes 786432 | tf_op jit(solution)/shard_map/select/pallas_call | solution.py:152
  37.6 18.1 %all-to-all-done.1 = f32[32,48,1,128]{3,1,2,0:T(8,128)S(1)} async-done(((f32[32,48,1,128]{3,1,2,0:T(8,128)}), f32[32,48,1,128]{3,1,2,0:T(8,128)S(1)}, u32[]{:S(2)}, u32[]{:S(2)}) %all-to-all-start.1) | async-done | bytes 786464 | tf_op jit(solution)/shard_map/all_to_all | solution.py:139
  55.7 1.5 %pool.1 = f32[128,2,128]{2,1,0:T(2,128)} custom-call(bf16[2,128,1536]{2,1,0:T(8,128)(2,1)S(1)} %select.4.refs_0_, f32[1536,128]{1,0:T(8,128)S(1)} %bitcast.18), custom_call_target="tpu_custom_call" | custom-call | tf_op jit(solution)/shard_map/pool/pallas_call | solution.py:161
  (7 shorter events, 0.1 us)
Async XLA Ops:
  1.4 33.7 %copy-start.1 = (s32[1,2,32,16]{2,3,1,0:T(8,128)S(1)}, s32[1,2,32,16]{2,3,1,0:T(8,128)}, u32[]{:S(2)}) copy-start(s32[1,2,32,16]{2,3,1,0:T(8,128)} %param.7) | copy-start | bytes 12292
  1.4 34.4 %copy-start.2 = (s32[128,2,8]{0,2,1:T(8,128)S(1)}, s32[128,2,8]{0,2,1:T(8,128)}, u32[]{:S(2)}) copy-start(s32[128,2,8]{0,2,1:T(8,128)} %param.9) | copy-start | bytes 24580
  25.1 0.7 %copy-start = (f32[32,17,1,128]{3,2,1,0:T(1,128)}, f32[32,17,1,128]{3,2,1,0:T(1,128)S(1)}, u32[]{:S(2)}) copy-start(f32[32,17,1,128]{3,2,1,0:T(1,128)S(1)} %all_to_all.10.refs_1_) | copy-start | bytes 835588
  32.5 23.2 %all-to-all-start.1 = ((f32[32,48,1,128]{3,1,2,0:T(8,128)}), f32[32,48,1,128]{3,1,2,0:T(8,128)S(1)}, u32[]{:S(2)}, u32[]{:S(2)}) async-start(f32[32,48,1,128]{3,1,2,0:T(8,128)} %bitcast.22), calls=%async_computation.1 | async-start | bytes 1572864 | tf_op jit(solution)/shard_map/all_to_all | solution.py:139

commit v3 on v2

--- a/solution.py
+++ b/solution.py
@@ -9,30 +9,29 @@
 AXES = ("gx", "gy")
 
 
-def push_hot(peers, tables, hot_each, rows_dev, base_ref, hot_ref, index_ref, table_ref, out_ref, sem):
-    chunk = tables * hot_each + 1
+def push_hot(peers, depth, rows_dev, me_ref, order_ref, starts_ref, hot_ref, index_ref, table_ref, out_ref, sem):
+    chunk = depth + 1
+    listed = hot_ref.shape[1]
     out_ref[...] = jnp.zeros_like(out_ref)
-    base = base_ref[0]
-
-    def one_peer(peer, count):
-        for t in range(tables):
-            for s in range(hot_each):
-                row = hot_ref[t, peer * hot_each + s] - base
-                mine = jnp.logical_and(row >= 0, row < rows_dev)
-
-                @pl.when(mine)
-                def _():
-                    pltpu.make_async_copy(
-                        table_ref.at[t * rows_dev + row],
-                        out_ref.at[peer * chunk + t * hot_each + s],
-                        sem,
-                    ).start()
-
-                count = count + mine.astype(jnp.int32)
-        out_ref[peer * chunk + chunk - 1] = index_ref[peer]
-        return count
-
-    count = lax.fori_loop(0, peers, one_peer, jnp.int32(0))
+    me = me_ref[0]
+    start = starts_ref[me]
+    count = starts_ref[me + 1] - start
+
+    def one_entry(r, carry):
+        place = start + r
+        entry = order_ref[place]
+        t = lax.div(entry, listed)
+        row = hot_ref[t, entry - t * listed] - me * rows_dev
+        pltpu.make_async_copy(
+            table_ref.at[t * rows_dev + row],
+            out_ref.at[lax.rem(place, peers) * chunk + lax.div(r, peers)],
+            sem,
+        ).start()
+        return carry
+
+    lax.fori_loop(0, count, one_entry, 0)
+    for peer in range(peers):
+        out_ref[peer * chunk + depth] = index_ref[peer]
 
     @pl.when(count > 0)
     def _():
@@ -41,9 +40,8 @@
         ).wait()
 
 
-def look_up(peers, tables, slots, hot_each, rows_dev, rows_ref, hot_ref, table_ref, out_ref, sem):
+def look_up(peers, tables, slots, depth, hot, rows_dev, me_ref, starts_ref, rows_ref, hot_ref, table_ref, out_ref, hot_sc, sem):
     cold = tables * slots
-    hot = tables * hot_each
     chunk = cold + hot
 
     def one_peer(peer, carry):
@@ -58,9 +56,24 @@
         return carry
 
     lax.fori_loop(0, peers, one_peer, 0)
-    total = hot_ref[0, pl.ds(0, hot)]
-    for peer in range(1, peers):
-        total = total + hot_ref[peer, pl.ds(0, hot)]
+    hot_sc[...] = jnp.zeros_like(hot_sc)
+    me = me_ref[0]
+
+    def one_owner(owner, carry):
+        start = starts_ref[owner]
+        count = starts_ref[owner + 1] - start
+        first = lax.rem(me + hot * peers - start, peers)
+        for d in range(depth):
+            r = first + d * peers
+
+            @pl.when(r < count)
+            def _():
+                hot_sc[lax.div(start + r, peers)] = hot_ref[owner, d]
+
+        return carry
+
+    lax.fori_loop(0, peers, one_owner, 0)
+    total = hot_sc[...]
     for peer in range(peers):
         out_ref[pl.ds(peer * chunk + cold, hot)] = total
     pltpu.make_async_copy(
@@ -99,11 +112,19 @@
     slots = cold_rows.shape[3]
     batch = hot_ids.shape[0]
     hot_count = hot_rows.shape[1]
-    hot_each = -(-hot_count // peers)
+    entries = table_count * hot_count
+    hot = -(-entries // peers)
     cold = table_count * slots
-    hot = table_count * hot_each
-    base = (lax.axis_index(AXES) * rows_dev).astype(jnp.int32).reshape(1)
-    hot_rows = jnp.pad(hot_rows, ((0, 0), (0, hot_each * peers - hot_count)), constant_values=-1)
+    me = lax.axis_index(AXES).astype(jnp.int32).reshape(1)
+
+    owner = lax.div(hot_rows.reshape(-1), jnp.int32(rows_dev))
+    key = owner * entries + jnp.arange(entries, dtype=jnp.int32)
+    rank = jnp.sum((key[None, :] < key[:, None]).astype(jnp.int32), axis=1)
+    position = jnp.arange(hot * peers, dtype=jnp.int32)
+    order = jnp.sum(jnp.where(rank[:, None] == position[None, :], jnp.arange(entries, dtype=jnp.int32)[:, None], 0), axis=0)
+    order = jnp.where(position < entries, order, entries)
+    starts = jnp.sum((owner[None, :] < jnp.arange(peers + 1, dtype=jnp.int32)[:, None]).astype(jnp.int32), axis=1)
+    most = jnp.max(starts[1:] - starts[:-1])
     flat = tables.reshape(table_count * rows_dev, 1, width)
     lanes = -(-cold // width)
     assert lanes == 1
@@ -115,39 +136,41 @@
     anywhere = pl.BlockSpec(memory_space=pl.ANY)
     small = pltpu.CompilerParams(vmem_limit_bytes=24 * 1024 * 1024)
 
-    first = pl.pallas_call(
-        lambda *refs: push_hot(peers, table_count, hot_each, rows_dev, *refs),
-        out_shape=jax.ShapeDtypeStruct((peers * (hot + 1), 1, width), jnp.float32),
-        in_specs=[smem, smem, vmem, anywhere],
-        out_specs=vmem,
-        scratch_shapes=[pltpu.SemaphoreType.DMA],
-        name="push_hot",
-    )(base, hot_rows, wanted, flat)
-    first = first.reshape(peers, hot + 1, 1, width)
-    first = lax.all_to_all(first, AXES, split_axis=0, concat_axis=0, tiled=True)
-    asked = first[:, hot, 0, :cold].astype(jnp.int32)
-
-    second = pl.pallas_call(
-        lambda *refs: look_up(peers, table_count, slots, hot_each, rows_dev, *refs),
-        out_shape=jax.ShapeDtypeStruct((peers * (cold + hot), 1, width), jnp.float32),
-        in_specs=[smem, vmem, anywhere],
-        out_specs=vmem,
-        scratch_shapes=[pltpu.SemaphoreType.DMA],
-        name="look_up",
-    )(asked, first, flat)
+    def gather(depth):
+        first = pl.pallas_call(
+            lambda *refs: push_hot(peers, depth, rows_dev, *refs),
+            out_shape=jax.ShapeDtypeStruct((peers * (depth + 1), 1, width), jnp.float32),
+            in_specs=[smem] * 4 + [vmem, anywhere],
+            out_specs=vmem,
+            scratch_shapes=[pltpu.SemaphoreType.DMA],
+            name="push_hot",
+        )(me, order, starts, hot_rows, wanted, flat)
+        first = first.reshape(peers, depth + 1, 1, width)
+        first = lax.all_to_all(first, AXES, split_axis=0, concat_axis=0, tiled=True)
+        asked = first[:, depth, 0, :cold].astype(jnp.int32)
+        return pl.pallas_call(
+            lambda *refs: look_up(peers, table_count, slots, depth, hot, rows_dev, *refs),
+            out_shape=jax.ShapeDtypeStruct((peers * (cold + hot), 1, width), jnp.float32),
+            in_specs=[smem] * 3 + [vmem, anywhere],
+            out_specs=vmem,
+            scratch_shapes=[pltpu.VMEM((hot, 1, width), jnp.float32), pltpu.SemaphoreType.DMA],
+            name="look_up",
+        )(me, starts, asked, first, flat)
+
+    narrow = min(2, hot)
+    second = lax.cond(most <= narrow * peers, lambda: gather(narrow), lambda: gather(hot))
     second = second.reshape(peers, cold + hot, 1, width)
     second = lax.all_to_all(second, AXES, split_axis=0, concat_axis=0, tiled=True)
     second = second.reshape(peers * (cold + hot), width)
 
-    slot_table = jnp.arange(cold + hot, dtype=jnp.int32)
     bags = []
     names = []
+    spread = jnp.transpose(order.reshape(hot, peers))
     for t in range(table_count):
         bags.append(jnp.pad(cold_bags[0, t], ((0, 0), (t * slots, cold + hot - (t + 1) * slots)), constant_values=-1).reshape(-1))
-        place = slot_table - cold - t * hot_each
-        inside = jnp.logical_and(place >= 0, place < hot_each)
-        peer = jnp.arange(peers, dtype=jnp.int32)[:, None]
-        names.append(jnp.where(inside[None, :], peer * hot_each + place[None, :], -1).reshape(-1))
+        name = spread - t * hot_count
+        name = jnp.where(jnp.logical_and(name >= 0, name < hot_count), name, -1)
+        names.append(jnp.pad(name, ((0, 0), (cold, 0)), constant_values=-1).reshape(-1))
     count = peers * (cold + hot)
     picks = pl.pallas_call(
         lambda *refs: select(table_count, *refs),

time: 57.5 us -> 53.6 us (0.932)
  blocking collectives: 18.4 us -> 14.7 us
  Pallas kernels: 14.9 us -> 11.9 us
  other arithmetic: 1.5 us -> 2.65 us
  local copies, waits for them, and re-layouts: 1.45 us -> 2.47 us
  between operations: 0.13 us -> 0.77 us
    all_to_all x1, blocking collectives: 18.4 us -> 14.7 us  [gather(): first = lax.all_to_all(first, AXES, split_axis=0, concat_axis=0, tiled=True)]
    pallas_call x2, Pallas kernels: 11.9 us -> 8.86 us  [the longest x1 6.64 us: gather(): pl.pallas_call(lambda *refs: look_up(peers, table_count, slots, depth, ho...]
    another operation x0 -> x3, local copies, waits for them, and re-layouts: none -> 0.84 us
    unnamed x9 -> x10, local copies, waits for them, and re-layouts: 0.33 us -> 1.12 us
    reduce_max x0 -> x1, other arithmetic: none -> 0.71 us  [body(): most = jnp.max(starts[1:] - starts[:-1])]
    pad x1, local copies, waits for them, and re-layouts: 0.62 us -> 0.01 us  [body(): wanted = jnp.pad(wanted, ((0, 0), (0, 0), (0, width - cold)))]
  transfers between devices with their start and end apart: 1 -> 1, of which waited for: 1 -> 1; matrix products, arithmetic and copies ran while one was open for 1% -> 2% of each run, Pallas kernels for 3% -> 3%
where the time goes in v3:
time: 53.6 us; the launch traced here: 53 us
  waiting for transfers between devices  17.8 us (33%)
  blocking collectives  14.7 us (27%)
  Pallas kernels  11.9 us (22%)
  other arithmetic  2.65 us (5%)
  starting transfers between devices  2.64 us (5%)
  local copies, waits for them, and re-layouts  2.47 us (5%)
  between operations  0.77 us (1%)
    all_to_all x1, waiting for transfers between devices, body(): lax.all_to_all(second, AXES, split_axis=0, concat_axis=0, tiled=True)  17.8 us
    all_to_all x1, blocking collectives, gather(): first = lax.all_to_all(first, AXES, split_axis=0, concat_axis=0, tiled=True)  14.7 us
    pallas_call x1, Pallas kernels, gather(): pl.pallas_call(lambda *refs: look_up(peers, table_count, slots, depth, ho...  6.64 us
    all_to_all x1, starting transfers between devices, body(): lax.all_to_all(second, AXES, split_axis=0, concat_axis=0, tiled=True)  2.64 us
    pallas_call x1, Pallas kernels, gather(): pl.pallas_call(lambda *refs: push_hot(peers, depth, rows_dev, *refs), out...  2.23 us
    pallas_call x1, Pallas kernels, body(): pl.pallas_call(lambda *refs: select(table_count, *refs), out_shape=jax.Sh...  1.54 us
    pallas_call x1, Pallas kernels, body(): pl.pallas_call(lambda *refs: pool(table_count, *refs), out_shape=jax.Shap...  1.47 us
    unnamed x10, local copies, waits for them, and re-layouts  1.12 us
  transfers between devices with their start and end apart: 1, of which 1 were waited for; matrix products, arithmetic and copies ran while one was open for 2% of the time, Pallas kernels for 3%

profile of v3, /device:TPU:0, one launch (start us, length us, event | category | flops | bytes accessed | tf_op | source)
XLA Modules:
  0.0 53.0 jit_solution(2185342904496985419)
XLA Ops:
  0.0 0.7 %copy.35 = s32[1,2,2,128]{3,1,2,0:T(2,128)S(1)} copy(s32[1,2,2,128]{3,2,1,0:T(2,128)} %bitcast.42) | data formatting | bytes 4096
  0.7 0.1 convert_reduce_fusion.1
  0.8 0.7 %subtract_reduce_fusion = s32[]{:T(128)} fusion(s32[33]{0:T(128)S(1)} %convert_reduce_fusion.1), kind=kLoop, calls=%fused_computation.25 | loop fusion | flops 63 | bytes 260 | tf_op jit(solution)/shard_map/reduce_max | solution.py:127
  2.2 0.2 convert_reduce_fusion
  2.4 0.2 select_reduce_fusion
  2.6 0.7 %convert_element_type.44 = f32[1,2,32,16]{2,3,1,0:T(8,128)S(1)} convert(s32[1,2,32,16]{2,3,1,0:T(8,128)} %param.8) | non-fusion elementwise | flops 1024 | bytes 8192 | tf_op jit(solution)/shard_map/convert_element_type | solution.py:131
  3.4 0.0 copy-start.2
  3.4 0.0 copy-start.3
  3.4 24.9 %conditional.1 = (f32[1536,1,128]{2,1,0:T(1,128)}) conditional(s32[]{:T(128)} %convert_element_type.43, (s32[1]{0:T(128)}, s32[512]{0:T(512)S(1)}, s32[33]{0:T(128)S(1)}, s32[2,256]{1,0:T(2,128)}, f32[32,1,128]{0,2,1:T(8,128)S(1)}, /*index=5*/f32[16384,1,128]{2,1,0:T(1,128)}) %tuple.24, (s32[1]{0:T(128)}, s32[512]{0:T(512)S(1)}, s32[33]{0:T(128)S(1)}, ...), branch_computations={%region_4.5_spmd, %region_5.6_spmd} | conditional | flops 1024 | bytes 1712164 | solution.py:161
  3.4 0.7 %copy.30.refs_4_ = f32[32,1,128]{2,1,0:T(1,128)} copy(f32[32,1,128]{0,2,1:T(8,128)S(1)} %get-tuple-element.78) | data formatting | bytes 32768 | tf_op jit(solution)/shard_map
  4.1 2.2 %push_hot.3 = f32[96,1,128]{2,1,0:T(1,128)} custom-call(s32[1]{0:T(128)} %get-tuple-element.38.refs_0_, s32[512]{0:T(512)S(1)} %get-tuple-element.40.refs_1_, s32[33]{0:T(128)S(1)} %get-tuple-element.39.refs_2_.refs_1_, s32[2,256]{1,0:T(2,128)} %get-tuple-element.41.refs_3_, f32[32,1,128]{2,1,0:T(1,128)} %copy.30.refs_4_, ...), custom_call_target="tpu_custom_call" | custom-call | tf_op jit(solution)/shard_map/cond/branch_1_fun/push_hot/pallas_call | solution.py:140
  6.3 14.7 %all_to_all.14.refs_3_ = f32[32,3,1,128]{3,2,1,0:T(1,128)S(1)} all-to-all(f32[32,3,1,128]{3,2,1,0:T(1,128)} %bitcast.38), channel_id=1, replica_groups=mesh['gx'=4,'gy'=8] {'gx','gy'}, dimensions={0} | all-to-all | bytes 98304 | tf_op jit(solution)/shard_map/cond/branch_1_fun/all_to_all | solution.py:149
  21.0 0.0 copy-start.1
  21.0 0.6 %slice_convert_fusion.1 = s32[32,1,1,32]{3,2,1,0:T(1,128)} fusion(f32[32,3,1,128]{3,2,1,0:T(1,128)S(1)} %all_to_all.14.refs_3_), kind=kLoop, calls=%fused_computation.1 | loop fusion | flops 1024 | bytes 8192 | tf_op jit(solution)/shard_map/cond/branch_1_fun/convert_element_type | solution.py:150
  21.6 0.0 copy-done.1
  21.6 6.6 %look_up.3 = f32[1536,1,128]{2,1,0:T(1,128)} custom-call(s32[1]{0:T(128)} %get-tuple-element.38.refs_0_, s32[33]{0:T(128)S(1)} %get-tuple-element.39.refs_2_.refs_1_, s32[32,32]{1,0:T(8,128)} %bitcast.40, f32[32,3,1,128]{3,2,1,0:T(1,128)} %copy-done.1, f32[16384,1,128]{2,1,0:T(1,128)} %get-tuple-element.43.refs_5_.refs_4_), custom_call_target="tpu_custom_call" | custom-call | tf_op jit(solution)/shard_map/cond/branch_1_fun/look_up/pallas_call | solution.py:151
  28.3 2.6 %all-to-all-start.2 = ((f32[32,48,1,128]{3,1,2,0:T(8,128)}), f32[32,48,1,128]{3,1,2,0:T(8,128)S(1)}, u32[]{:S(2)}, u32[]{:S(2)}) async-start(f32[32,48,1,128]{3,1,2,0:T(8,128)} %bitcast.13), calls=%async_computation.2 | async-start | bytes 1572864 | tf_op jit(solution)/shard_map/all_to_all | solution.py:163
  30.9 0.1 reduce_sum.31
  31.0 0.1 copy.33
  31.1 0.1 pad.21.clone
  31.1 0.1 stack_reshape.14
  31.2 0.1 copy.34
  31.3 0.1 pad.22.clone
  31.4 0.1 stack_reshape.15
  31.5 0.0 copy-done.2
  31.5 0.1 copy.31
  31.6 0.1 stack_reshape.12
  31.7 0.1 copy.32
  31.8 0.1 pad.20.clone
  31.8 0.1 stack_reshape.13
  31.9 0.0 copy-done.3
  31.9 0.1 copy.28
  32.1 1.5 %select.30.refs_0_ = bf16[2,128,1536]{2,1,0:T(8,128)(2,1)S(1)} custom-call(s32[2,1536]{1,0:T(2,128)S(1)} %get-tuple-element.86.refs_0_, s32[2,1536]{1,0:T(2,128)S(1)} %get-tuple-element.87.refs_1_, s32[2,128,8]{2,1,0:T(8,128)S(1)} %bitcast.34), custom_call_target="tpu_custom_call" | custom-call | flops 15728640 | bytes 786432 | tf_op jit(solution)/shard_map/select/pallas_call | solution.py:175
  33.6 17.8 %all-to-all-done.2 = f32[32,48,1,128]{3,1,2,0:T(8,128)S(1)} async-done(((f32[32,48,1,128]{3,1,2,0:T(8,128)}), f32[32,48,1,128]{3,1,2,0:T(8,128)S(1)}, u32[]{:S(2)}, u32[]{:S(2)}) %all-to-all-start.2) | async-done | bytes 786464 | tf_op jit(solution)/shard_map/all_to_all | solution.py:163
  51.5 1.5 %pool.1 = f32[128,2,128]{2,1,0:T(2,128)} custom-call(bf16[2,128,1536]{2,1,0:T(8,128)(2,1)S(1)} %select.30.refs_0_, f32[1536,128]{1,0:T(8,128)S(1)} %bitcast.33), custom_call_target="tpu_custom_call" | custom-call | tf_op jit(solution)/shard_map/pool/pallas_call | solution.py:184
  (7 shorter events, 0.1 us)
Async XLA Ops:
  3.4 28.1 %copy-start.2 = (s32[1,2,32,16]{2,3,1,0:T(8,128)S(1)}, s32[1,2,32,16]{2,3,1,0:T(8,128)}, u32[]{:S(2)}) copy-start(s32[1,2,32,16]{2,3,1,0:T(8,128)} %param.9) | copy-start | bytes 12292
  3.4 28.6 %copy-start.3 = (s32[128,2,8]{0,2,1:T(8,128)S(1)}, s32[128,2,8]{0,2,1:T(8,128)}, u32[]{:S(2)}) copy-start(s32[128,2,8]{0,2,1:T(8,128)} %param.11) | copy-start | bytes 24580
  21.0 0.6 %copy-start.1 = (f32[32,3,1,128]{3,2,1,0:T(1,128)}, f32[32,3,1,128]{3,2,1,0:T(1,128)S(1)}, u32[]{:S(2)}) copy-start(f32[32,3,1,128]{3,2,1,0:T(1,128)S(1)} %all_to_all.14.refs_3_) | copy-start | bytes 147460 | tf_op jit(solution)/shard_map/cond
  28.3 23.2 %all-to-all-start.2 = ((f32[32,48,1,128]{3,1,2,0:T(8,128)}), f32[32,48,1,128]{3,1,2,0:T(8,128)S(1)}, u32[]{:S(2)}, u32[]{:S(2)}) async-start(f32[32,48,1,128]{3,1,2,0:T(8,128)} %bitcast.13), calls=%async_computation.2 | async-start | bytes 1572864 | tf_op jit(solution)/shard_map/all_to_all | solution.py:163

commit v4 on v3

--- a/solution.py
+++ b/solution.py
@@ -52,7 +52,7 @@
                     table_ref.at[t * rows_dev + row],
                     out_ref.at[peer * chunk + t * slots + c],
                     sem,
-                ).start()
+                ).start(priority=c % 2)
         return carry
 
     lax.fori_loop(0, peers, one_peer, 0)

time: 53.6 us -> 51.9 us (0.968)
  Pallas kernels: 11.9 us -> 10.4 us
    pallas_call x1, Pallas kernels: 6.64 us -> 5.1 us  [gather(): pl.pallas_call(lambda *refs: look_up(peers, table_count, slots, depth, ho...]
where the time goes in v4:
time: 51.9 us; the launch traced here: 51.4 us
  waiting for transfers between devices  17.8 us (34%)
  blocking collectives  14.7 us (28%)
  Pallas kernels  10.4 us (20%)
  other arithmetic  2.65 us (5%)
  starting transfers between devices  2.64 us (5%)
  local copies, waits for them, and re-layouts  2.47 us (5%)
  between operations  0.77 us (1%)
    all_to_all x1, waiting for transfers between devices, body(): lax.all_to_all(second, AXES, split_axis=0, concat_axis=0, tiled=True)  17.8 us
    all_to_all x1, blocking collectives, gather(): first = lax.all_to_all(first, AXES, split_axis=0, concat_axis=0, tiled=True)  14.7 us
    pallas_call x1, Pallas kernels, gather(): pl.pallas_call(lambda *refs: look_up(peers, table_count, slots, depth, ho...  5.1 us
    all_to_all x1, starting transfers between devices, body(): lax.all_to_all(second, AXES, split_axis=0, concat_axis=0, tiled=True)  2.64 us
    pallas_call x1, Pallas kernels, gather(): pl.pallas_call(lambda *refs: push_hot(peers, depth, rows_dev, *refs), out...  2.24 us
    pallas_call x1, Pallas kernels, body(): pl.pallas_call(lambda *refs: select(table_count, *refs), out_shape=jax.Sh...  1.54 us
    pallas_call x1, Pallas kernels, body(): pl.pallas_call(lambda *refs: pool(table_count, *refs), out_shape=jax.Shap...  1.48 us
    unnamed x10, local copies, waits for them, and re-layouts  1.12 us
  transfers between devices with their start and end apart: 1, of which 1 were waited for; matrix products, arithmetic and copies ran while one was open for 2% of the time, Pallas kernels for 3%

profile of v4, /device:TPU:0, one launch (start us, length us, event | category | flops | bytes accessed | tf_op | source)
XLA Modules:
  0.0 51.4 jit_solution(13906402212815784489)
XLA Ops:
  0.0 0.7 %copy.35 = s32[1,2,2,128]{3,1,2,0:T(2,128)S(1)} copy(s32[1,2,2,128]{3,2,1,0:T(2,128)} %bitcast.42) | data formatting | bytes 4096
  0.7 0.1 convert_reduce_fusion.1
  0.8 0.7 %subtract_reduce_fusion = s32[]{:T(128)} fusion(s32[33]{0:T(128)S(1)} %convert_reduce_fusion.1), kind=kLoop, calls=%fused_computation.25 | loop fusion | flops 63 | bytes 260 | tf_op jit(solution)/shard_map/reduce_max | solution.py:127
  2.2 0.2 convert_reduce_fusion
  2.4 0.2 select_reduce_fusion
  2.6 0.7 %convert_element_type.44 = f32[1,2,32,16]{2,3,1,0:T(8,128)S(1)} convert(s32[1,2,32,16]{2,3,1,0:T(8,128)} %param.8) | non-fusion elementwise | flops 1024 | bytes 8192 | tf_op jit(solution)/shard_map/convert_element_type | solution.py:131
  3.4 0.0 copy-start.2
  3.4 0.0 copy-start.3
  3.4 23.3 %conditional.1 = (f32[1536,1,128]{2,1,0:T(1,128)}) conditional(s32[]{:T(128)} %convert_element_type.43, (s32[1]{0:T(128)}, s32[512]{0:T(512)S(1)}, s32[33]{0:T(128)S(1)}, s32[2,256]{1,0:T(2,128)}, f32[32,1,128]{0,2,1:T(8,128)S(1)}, /*index=5*/f32[16384,1,128]{2,1,0:T(1,128)}) %tuple.24, (s32[1]{0:T(128)}, s32[512]{0:T(512)S(1)}, s32[33]{0:T(128)S(1)}, ...), branch_computations={%region_4.5_spmd, %region_5.6_spmd} | conditional | flops 1024 | bytes 1712164 | solution.py:161
  3.4 0.7 %copy.30.refs_4_ = f32[32,1,128]{2,1,0:T(1,128)} copy(f32[32,1,128]{0,2,1:T(8,128)S(1)} %get-tuple-element.78) | data formatting | bytes 32768 | tf_op jit(solution)/shard_map
  4.1 2.2 %push_hot.3 = f32[96,1,128]{2,1,0:T(1,128)} custom-call(s32[1]{0:T(128)} %get-tuple-element.38.refs_0_, s32[512]{0:T(512)S(1)} %get-tuple-element.40.refs_1_, s32[33]{0:T(128)S(1)} %get-tuple-element.39.refs_2_.refs_1_, s32[2,256]{1,0:T(2,128)} %get-tuple-element.41.refs_3_, f32[32,1,128]{2,1,0:T(1,128)} %copy.30.refs_4_, ...), custom_call_target="tpu_custom_call" | custom-call | tf_op jit(solution)/shard_map/cond/branch_1_fun/push_hot/pallas_call | solution.py:140
  6.3 14.7 %all_to_all.14.refs_3_ = f32[32,3,1,128]{3,2,1,0:T(1,128)S(1)} all-to-all(f32[32,3,1,128]{3,2,1,0:T(1,128)} %bitcast.38), channel_id=1, replica_groups=mesh['gx'=4,'gy'=8] {'gx','gy'}, dimensions={0} | all-to-all | bytes 98304 | tf_op jit(solution)/shard_map/cond/branch_1_fun/all_to_all | solution.py:149
  21.0 0.0 copy-start.1
  21.0 0.6 %slice_convert_fusion.1 = s32[32,1,1,32]{3,2,1,0:T(1,128)} fusion(f32[32,3,1,128]{3,2,1,0:T(1,128)S(1)} %all_to_all.14.refs_3_), kind=kLoop, calls=%fused_computation.1 | loop fusion | flops 1024 | bytes 8192 | tf_op jit(solution)/shard_map/cond/branch_1_fun/convert_element_type | solution.py:150
  21.6 0.0 copy-done.1
  21.6 5.1 %look_up.3 = f32[1536,1,128]{2,1,0:T(1,128)} custom-call(s32[1]{0:T(128)} %get-tuple-element.38.refs_0_, s32[33]{0:T(128)S(1)} %get-tuple-element.39.refs_2_.refs_1_, s32[32,32]{1,0:T(8,128)} %bitcast.40, f32[32,3,1,128]{3,2,1,0:T(1,128)} %copy-done.1, f32[16384,1,128]{2,1,0:T(1,128)} %get-tuple-element.43.refs_5_.refs_4_), custom_call_target="tpu_custom_call" | custom-call | tf_op jit(solution)/shard_map/cond/branch_1_fun/look_up/pallas_call | solution.py:151
  26.7 2.6 %all-to-all-start.2 = ((f32[32,48,1,128]{3,1,2,0:T(8,128)}), f32[32,48,1,128]{3,1,2,0:T(8,128)S(1)}, u32[]{:S(2)}, u32[]{:S(2)}) async-start(f32[32,48,1,128]{3,1,2,0:T(8,128)} %bitcast.13), calls=%async_computation.2 | async-start | bytes 1572864 | tf_op jit(solution)/shard_map/all_to_all | solution.py:163
  29.4 0.1 reduce_sum.31
  29.5 0.1 copy.33
  29.5 0.1 pad.21.clone
  29.6 0.1 stack_reshape.14
  29.7 0.1 copy.34
  29.8 0.1 pad.22.clone
  29.9 0.1 stack_reshape.15
  30.0 0.0 copy-done.2
  30.0 0.1 copy.31
  30.1 0.1 stack_reshape.12
  30.1 0.1 copy.32
  30.2 0.1 pad.20.clone
  30.3 0.1 stack_reshape.13
  30.4 0.0 copy-done.3
  30.4 0.1 copy.28
  30.6 1.5 %select.30.refs_0_ = bf16[2,128,1536]{2,1,0:T(8,128)(2,1)S(1)} custom-call(s32[2,1536]{1,0:T(2,128)S(1)} %get-tuple-element.86.refs_0_, s32[2,1536]{1,0:T(2,128)S(1)} %get-tuple-element.87.refs_1_, s32[2,128,8]{2,1,0:T(8,128)S(1)} %bitcast.34), custom_call_target="tpu_custom_call" | custom-call | flops 15728640 | bytes 786432 | tf_op jit(solution)/shard_map/select/pallas_call | solution.py:175
  32.1 17.8 %all-to-all-done.2 = f32[32,48,1,128]{3,1,2,0:T(8,128)S(1)} async-done(((f32[32,48,1,128]{3,1,2,0:T(8,128)}), f32[32,48,1,128]{3,1,2,0:T(8,128)S(1)}, u32[]{:S(2)}, u32[]{:S(2)}) %all-to-all-start.2) | async-done | bytes 786464 | tf_op jit(solution)/shard_map/all_to_all | solution.py:163
  49.9 1.5 %pool.1 = f32[128,2,128]{2,1,0:T(2,128)} custom-call(bf16[2,128,1536]{2,1,0:T(8,128)(2,1)S(1)} %select.30.refs_0_, f32[1536,128]{1,0:T(8,128)S(1)} %bitcast.33), custom_call_target="tpu_custom_call" | custom-call | tf_op jit(solution)/shard_map/pool/pallas_call | solution.py:184
  (7 shorter events, 0.1 us)
Async XLA Ops:
  3.4 26.6 %copy-start.2 = (s32[1,2,32,16]{2,3,1,0:T(8,128)S(1)}, s32[1,2,32,16]{2,3,1,0:T(8,128)}, u32[]{:S(2)}) copy-start(s32[1,2,32,16]{2,3,1,0:T(8,128)} %param.9) | copy-start | bytes 12292
  3.4 27.0 %copy-start.3 = (s32[128,2,8]{0,2,1:T(8,128)S(1)}, s32[128,2,8]{0,2,1:T(8,128)}, u32[]{:S(2)}) copy-start(s32[128,2,8]{0,2,1:T(8,128)} %param.11) | copy-start | bytes 24580
  21.0 0.6 %copy-start.1 = (f32[32,3,1,128]{3,2,1,0:T(1,128)}, f32[32,3,1,128]{3,2,1,0:T(1,128)S(1)}, u32[]{:S(2)}) copy-start(f32[32,3,1,128]{3,2,1,0:T(1,128)S(1)} %all_to_all.14.refs_3_) | copy-start | bytes 147460 | tf_op jit(solution)/shard_map/cond
  26.7 23.2 %all-to-all-start.2 = ((f32[32,48,1,128]{3,1,2,0:T(8,128)}), f32[32,48,1,128]{3,1,2,0:T(8,128)S(1)}, u32[]{:S(2)}, u32[]{:S(2)}) async-start(f32[32,48,1,128]{3,1,2,0:T(8,128)} %bitcast.13), calls=%async_computation.2 | async-start | bytes 1572864 | tf_op jit(solution)/shard_map/all_to_all | solution.py:163
